TPU v7x, 32 devices: a whole 2x2x4 slice. The times are simulated.
32 devices in a mesh: expert: 4 (over x, core), shard: 8 (over z, y).
Axes of the slice: x: 2, y: 2, z: 4, core: 2. Of those that a mesh axis runs over, the one named last changes fastest.
Arguments:
- master_gate: float32 [128, 2048, 768], P('expert', 'shard'), may hold values from -0.125 to 0.125
- master_up: float32 [128, 2048, 768], P('expert', 'shard'), may hold values from -0.125 to 0.125
- router_weight: float32 [2048, 128], P('shard', 'expert'), may hold values from -0.125 to 0.125
- router_gain: float32 [2048], P('shard'), may hold values from 0.25 to 1.75
Outputs:
- final_gate: bfloat16 [128, 768, 2048], P('expert', 'shard')
- final_up: bfloat16 [128, 768, 2048], P('expert', 'shard')
- serve_router: bfloat16 [2048, 128], replicated
All inputs are finite; a program needn't handle non-finite values.
Results may differ from a plain program's by a relative error of at most 0.001.
Values may be sent and summed in bfloat16 or wider, within the bound.
A program may use at most 192 MiB of HBM per device.

v0:
```python
import jax
import jax.numpy as jnp
from jax import lax
from jax.sharding import PartitionSpec as P


def per_device(master_gate, master_up, router_weight, router_gain):
    narrow_gate, narrow_up = (master_gate.astype(jnp.bfloat16), master_up.astype(jnp.bfloat16))
    final_gate, final_up = (
        lax.all_to_all(narrow_gate, "shard", split_axis=2, concat_axis=1, tiled=True),
        lax.all_to_all(narrow_up, "shard", split_axis=2, concat_axis=1, tiled=True),
    )
    final_gate = jnp.transpose(final_gate, (0, 2, 1))
    final_up = jnp.transpose(final_up, (0, 2, 1))
    part_router = (router_weight * router_gain[:, None]).astype(jnp.bfloat16)
    row_router = lax.all_gather(part_router, "shard", axis=0, tiled=True)
    serve_router = lax.all_gather(row_router, "expert", axis=1, tiled=True)
    return (final_gate, final_up, serve_router)


def solution(mesh):
    placed = (
        P("expert", "shard", None),
        P("expert", "shard", None),
        P("shard", "expert"),
        P("shard"),
    )
    return jax.shard_map(
        per_device,
        mesh=mesh,
        in_specs=placed,
        out_specs=(P("expert", "shard", None), P("expert", "shard", None), P()),
        check_vma=False,
    )
```

profile of v0, /device:TPU:0, one launch (start us, length us, event | category | flops | bytes accessed | tf_op | source)
XLA Modules:
  0.0 675.1 jit_solution(9694848877935165058)
XLA Ops:
  0.6 21.3 %copy.18 = bf16[32,256,768]{1,0,2:T(8,128)(2,1)} copy(f32[32,256,768]{2,1,0:T(8,128)} %param.4) | data formatting | bytes 37748736 | tf_op args[0]
  21.9 7.3 %all-to-all-start = ((bf16[32,256,768]{1,0,2:T(8,128)(2,1)}), bf16[32,256,768]{1,0,2:T(8,128)(2,1)}, u32[]{:S(2)}, u32[]{:S(2)}) async-start(bf16[32,256,768]{1,0,2:T(8,128)(2,1)} %copy.18), calls=%async_computation | async-start | bytes 25165824 | tf_op jit(solution)/shard_map/all_to_all | solution.py:10
  29.2 21.4 %copy.21 = bf16[32,256,768]{1,0,2:T(8,128)(2,1)} copy(f32[32,256,768]{2,1,0:T(8,128)} %param.5) | data formatting | bytes 37748736 | tf_op args[1]
  50.6 0.0 copy-start
  50.6 0.0 copy-start.1
  50.6 251.6 %all-to-all-done = bf16[32,256,768]{1,0,2:T(8,128)(2,1)} async-done(((bf16[32,256,768]{1,0,2:T(8,128)(2,1)}), bf16[32,256,768]{1,0,2:T(8,128)(2,1)}, u32[]{:S(2)}, u32[]{:S(2)}) %all-to-all-start) | async-done | bytes 12582944 | tf_op jit(solution)/shard_map/all_to_all | solution.py:10
  302.3 5.3 all-to-all-start.1
  307.6 0.0 copy-done
  307.6 0.0 copy-done.1
  307.7 292.2 %all_gather.6 = bf16[2048,32]{0,1:T(8,128)(2,1)S(1)} all-gather(bf16[256,32]{0,1:T(8,128)(2,1)S(1)} %multiply_convert_fusion), channel_id=1, replica_groups=mesh['expert'=4,'shard'=8] {'shard'}, dimensions={0}, use_global_device_ids=true | all-gather | bytes 147456 | tf_op jit(solution)/shard_map/all_gather | solution.py:16
  599.9 7.2 %all_gather.7 = bf16[2048,128]{0,1:T(8,128)(2,1)S(1)} all-gather(bf16[2048,32]{0,1:T(8,128)(2,1)S(1)} %all_gather.6), channel_id=1, replica_groups=mesh['expert'=4,'shard'=8] {'expert'}, dimensions={1}, use_global_device_ids=true | all-gather | bytes 655360 | tf_op jit(solution)/shard_map/all_gather | solution.py:17
  607.0 1.0 copy.24
  608.0 14.1 %copy.20 = bf16[32,8,256,96]{2,1,3,0:T(8,128)(2,1)} copy(bf16[32,8,256,96]{2,0,3,1:T(8,128)(2,1)} %bitcast.2) | data formatting | bytes 25165824 | tf_op jit(solution)/shard_map/all_to_all | solution.py:10
  622.1 19.5 %all_to_all.29 = bf16[32,2048,96]{1,2,0:T(8,128)(2,1)} reshape(bf16[32,8,256,96]{2,1,3,0:T(8,128)(2,1)} %copy.20) | data formatting | bytes 25165824 | tf_op jit(solution)/shard_map/all_to_all | solution.py:10
  641.6 0.0 all-to-all-done.1
  641.6 14.1 %copy.23 = bf16[32,8,256,96]{2,1,3,0:T(8,128)(2,1)} copy(bf16[32,8,256,96]{2,0,3,1:T(8,128)(2,1)} %bitcast.6) | data formatting | bytes 25165824 | tf_op jit(solution)/shard_map/all_to_all | solution.py:11
  655.7 19.5 %all_to_all.33 = bf16[32,2048,96]{1,2,0:T(8,128)(2,1)} reshape(bf16[32,8,256,96]{2,1,3,0:T(8,128)(2,1)} %copy.23) | data formatting | bytes 25165824 | tf_op jit(solution)/shard_map/all_to_all | solution.py:11
  (1 shorter events, 0.0 us)
Async XLA Ops:
  21.9 280.4 %all-to-all-start = ((bf16[32,256,768]{1,0,2:T(8,128)(2,1)}), bf16[32,256,768]{1,0,2:T(8,128)(2,1)}, u32[]{:S(2)}, u32[]{:S(2)}) async-start(bf16[32,256,768]{1,0,2:T(8,128)(2,1)} %copy.18), calls=%async_computation | async-start | bytes 25165824 | tf_op jit(solution)/shard_map/all_to_all | solution.py:10
  50.6 257.0 %copy-start = (f32[256,32]{0,1:T(8,128)S(1)}, f32[256,32]{0,1:T(8,128)}, u32[]{:S(2)}) copy-start(f32[256,32]{0,1:T(8,128)} %param.6) | copy-start | bytes 98308
  50.6 257.0 %copy-start.1 = (f32[256]{0:T(256)S(1)}, f32[256]{0:T(256)}, u32[]{:S(2)}) copy-start(f32[256]{0:T(256)} %param.7) | copy-start | bytes 3076
  302.3 339.3 %all-to-all-start.1 = ((bf16[32,256,768]{1,0,2:T(8,128)(2,1)}), bf16[32,256,768]{1,0,2:T(8,128)(2,1)}, u32[]{:S(2)}, u32[]{:S(2)}) async-start(bf16[32,256,768]{1,0,2:T(8,128)(2,1)} %copy.21), calls=%async_computation.1 | async-start | bytes 25165824 | tf_op jit(solution)/shard_map/all_to_all | solution.py:11
where the time goes:
time: 677 us; the launch traced here: 675 us
  blocking collectives  299 us (44%)
  waiting for transfers between devices  252 us (37%)
  local copies, waits for them, and re-layouts  111 us (16%)
  starting transfers between devices  12.7 us (2%)
    all_gather x1, blocking collectives, per_device(): row_router = lax.all_gather(part_router, 'shard', axis=0, tiled=True)  292 us
    all_to_all x1, waiting for transfers between devices, per_device(): lax.all_to_all(narrow_gate, 'shard', split_axis=2, concat_axis=1, tiled=T...  252 us
    unnamed x7, local copies, waits for them, and re-layouts  43.7 us
    all_to_all x2, local copies, waits for them, and re-layouts, per_device(): lax.all_to_all(narrow_up, 'shard', split_axis=2, concat_axis=1, tiled=True)  33.6 us
    all_to_all x2, local copies, waits for them, and re-layouts, per_device(): lax.all_to_all(narrow_gate, 'shard', split_axis=2, concat_axis=1, tiled=T...  33.5 us
  transfers between devices with their start and end apart: 2, of which 1 were waited for; matrix products, arithmetic and copies ran while one was open for 5% of the time, Pallas kernels for 0%

commit v1 on v0

--- a/solution.py
+++ b/solution.py
@@ -1,10 +1,20 @@
+import functools
+
 import jax
 import jax.numpy as jnp
 from jax import lax
+from jax.experimental import pallas as pl
+from jax.experimental.pallas import tpu as pltpu
 from jax.sharding import PartitionSpec as P
 
-
-def per_device(master_gate, master_up, router_weight, router_gain):
+NEAR = 1
+PAIR = 2
+CHUNK = 2
+SLOTS = 4
+LIMIT = 32
+
+
+def plain(master_gate, master_up, router_weight, router_gain):
     narrow_gate, narrow_up = (master_gate.astype(jnp.bfloat16), master_up.astype(jnp.bfloat16))
     final_gate, final_up = (
         lax.all_to_all(narrow_gate, "shard", split_axis=2, concat_axis=1, tiled=True),
@@ -18,6 +28,209 @@
     return (final_gate, final_up, serve_router)
 
 
+def kernel(
+    shards, groups, gate, up, weight, gain, out_gate, out_up, out_router,
+    held, coming, router, load_sem, own_sem, send_sem, recv_sem,
+    row_send, row_recv, column_send, column_recv,
+):
+    me, group = lax.axis_index("shard"), lax.axis_index("expert")
+    _, _, experts, rows, depth = held.shape
+    width = weight.shape[0]
+    chunks = experts // CHUNK
+    sources, outs = (gate, up), (out_gate, out_up)
+    mine = pl.ds(pl.multiple_of(me * depth, depth), depth)
+    my_part = pl.ds(pl.multiple_of(group * width, width), width)
+
+    barrier = pltpu.get_barrier_semaphore()
+    for step in range(1, shards):
+        pl.semaphore_signal(barrier, inc=1, device_id={"shard": lax.rem(me + step, shards)})
+    for step in range(1, groups):
+        pl.semaphore_signal(barrier, inc=1, device_id={"expert": lax.rem(group + step, groups)})
+
+    def load(which, expert):
+        slot = lax.rem(expert, SLOTS)
+        return pltpu.make_async_copy(sources[which].at[expert], coming.at[slot], load_sem.at[slot])
+
+    def own(which, span):
+        return pltpu.make_async_copy(
+            held.at[which, me, span], outs[which].at[span, :, mine], own_sem.at[which]
+        )
+
+    def send(which, peer, span):
+        return pltpu.make_async_remote_copy(
+            src_ref=held.at[which, peer, span],
+            dst_ref=outs[which].at[span, :, mine],
+            send_sem=send_sem.at[which, peer],
+            recv_sem=recv_sem.at[which, me],
+            device_id={"shard": peer},
+        )
+
+    def arrival(which, peer):
+        there = pl.ds(pl.multiple_of(peer * depth, depth), depth)
+        return pltpu.make_async_remote_copy(
+            src_ref=held.at[which, peer],
+            dst_ref=outs[which].at[:, :, there],
+            send_sem=send_sem.at[which, peer],
+            recv_sem=recv_sem.at[which, peer],
+            device_id={"shard": peer},
+        )
+
+    def row(peer):
+        return pltpu.make_async_remote_copy(
+            src_ref=router.at[me, my_part],
+            dst_ref=router.at[me, my_part],
+            send_sem=row_send.at[peer],
+            recv_sem=row_recv.at[me],
+            device_id={"shard": peer},
+        )
+
+    def row_arrival(peer):
+        return pltpu.make_async_remote_copy(
+            src_ref=router.at[peer, my_part],
+            dst_ref=router.at[peer, my_part],
+            send_sem=row_send.at[peer],
+            recv_sem=row_recv.at[peer],
+            device_id={"shard": peer},
+        )
+
+    def column(peer, of):
+        part = pl.ds(pl.multiple_of(of * width, width), width)
+        return pltpu.make_async_remote_copy(
+            src_ref=router.at[:, part],
+            dst_ref=router.at[:, part],
+            send_sem=column_send.at[peer],
+            recv_sem=column_recv.at[of],
+            device_id={"expert": peer},
+        )
+
+    def to_peers(least, most, act):
+        place, side = me // PAIR, lax.rem(me, PAIR)
+        for away in range(least, most + 1):
+            for turned in range(0 if away else 1, PAIR):
+                other = lax.rem(side + turned, PAIR)
+                if away == 0:
+                    act(place * PAIR + other)
+                    continue
+
+                @pl.when(place + away < shards // PAIR)
+                def _():
+                    act((place + away) * PAIR + other)
+
+                @pl.when(place >= away)
+                def _():
+                    act((place - away) * PAIR + other)
+
+    last = shards // PAIR - 1
+    for first in range(SLOTS):
+        load(0, first).start()
+    router[me, my_part] = (weight[...] * gain[...]).astype(jnp.bfloat16)
+
+    def turn(which, expert):
+        load(which, expert).wait()
+        block = coming[lax.rem(expert, SLOTS)].T.astype(jnp.bfloat16)
+        for peer in range(shards):
+            held[which, peer, expert] = block[peer * rows:(peer + 1) * rows]
+
+        @pl.when(expert + SLOTS < experts)
+        def _():
+            load(which, expert + SLOTS).start()
+
+    def turns(which, chunk):
+        @pl.loop(0, CHUNK)
+        def _(step):
+            turn(which, chunk * CHUNK + step)
+
+    def near(which, chunk):
+        span = pl.ds(chunk * CHUNK, CHUNK)
+        to_peers(0, NEAR, lambda peer: send(which, peer, span).start())
+        own(which, span).start()
+
+    for which in range(2):
+        turns(which, 0)
+        if which == 0:
+            pl.semaphore_wait(barrier, shards + groups - 2)
+            to_peers(0, last, lambda peer: row(peer).start())
+        else:
+            near(0, chunks - 1)
+
+        @pl.loop(1, chunks)
+        def _(chunk):
+            turns(which, chunk)
+            near(which, chunk - 1)
+
+        if which == 0:
+            for first in range(SLOTS):
+                load(1, first).start()
+    near(1, chunks - 1)
+    whole = pl.ds(0, experts)
+    for away in range(NEAR + 1, last + 1):
+        for which in range(2):
+            to_peers(away, away, lambda peer: send(which, peer, whole).start())
+
+    to_peers(0, last, lambda peer: row_arrival(peer).wait_recv())
+    for step in range(1, groups):
+        column(lax.rem(group + step, groups), group).start()
+    for step in range(1, groups):
+        peer = lax.rem(group + step, groups)
+        column(peer, peer).wait_recv()
+    for shard in range(shards):
+        out_router[shard * depth:(shard + 1) * depth] = router[shard].T
+    to_peers(0, last, lambda peer: row(peer).wait_send())
+    for step in range(1, groups):
+        column(lax.rem(group + step, groups), group).wait_send()
+
+    for which in range(2):
+        own(which, whole).wait()
+        to_peers(0, last, lambda peer: arrival(which, peer).wait())
+
+
+def put_out(gate, up, router, out_gate, out_up, out_router, sem):
+    copies = [
+        pltpu.make_async_copy(source, out, sem.at[at])
+        for at, (source, out) in enumerate(((gate, out_gate), (up, out_up), (router, out_router)))
+    ]
+    for copy in copies:
+        copy.start()
+    for copy in copies:
+        copy.wait()
+
+
+def per_device(shards, groups, master_gate, master_up, router_weight, router_gain):
+    experts, depth, inner = master_gate.shape
+    width = router_weight.shape[1]
+    rows = inner // shards
+    if shards % PAIR or depth % 128 or rows % 16 or width % 16 or experts % CHUNK or experts < 2 * CHUNK or (width * groups) % 128:
+        return plain(master_gate, master_up, router_weight, router_gain)
+    anywhere = pl.BlockSpec(memory_space=pl.ANY)
+    inside = pl.BlockSpec(memory_space=pltpu.VMEM)
+    final = pltpu.VMEM((experts, rows, shards * depth), jnp.bfloat16)
+    dma = pltpu.SemaphoreType.DMA
+    kept = pl.pallas_call(
+        functools.partial(kernel, shards, groups),
+        out_shape=(final, final, pltpu.VMEM((shards * depth, groups * width), jnp.bfloat16)),
+        in_specs=[anywhere, anywhere, inside, inside],
+        out_specs=(inside, inside, inside),
+        scratch_shapes=[
+            pltpu.VMEM((2, shards, experts, rows, depth), jnp.bfloat16),
+            pltpu.VMEM((SLOTS, depth, inner), jnp.float32),
+            pltpu.VMEM((shards, groups * width, depth), jnp.bfloat16),
+            dma((SLOTS,)), dma((2,)), dma((2, shards)), dma((2, shards)),
+            dma((shards,)), dma((shards,)), dma((groups,)), dma((groups,)),
+        ],
+        compiler_params=pltpu.CompilerParams(
+            collective_id=0, has_side_effects=True, vmem_limit_bytes=LIMIT * 2**20
+        ),
+    )(master_gate, master_up, router_weight.T, router_gain[None])
+    return pl.pallas_call(
+        put_out,
+        out_shape=tuple(jax.ShapeDtypeStruct(array.shape, array.dtype) for array in kept),
+        in_specs=[inside] * 3,
+        out_specs=(anywhere,) * 3,
+        scratch_shapes=[dma((3,))],
+        compiler_params=pltpu.CompilerParams(vmem_limit_bytes=2**20),
+    )(*kept)
+
+
 def solution(mesh):
     placed = (
         P("expert", "shard", None),
@@ -26,7 +239,7 @@
         P("shard"),
     )
     return jax.shard_map(
-        per_device,
+        functools.partial(per_device, mesh.shape["shard"], mesh.shape["expert"]),
         mesh=mesh,
         in_specs=placed,
         out_specs=(P("expert", "shard", None), P("expert", "shard", None), P()),

time: 677 us -> 561 us (0.83)
  Pallas kernels: 0 us -> 560 us
  blocking collectives: 299 us -> 0 us
  waiting for transfers between devices: 252 us -> 0 us
  local copies, waits for them, and re-layouts: 111 us -> 0 us
  starting transfers between devices: 12.7 us -> 0 us
    pallas_call x0 -> x2, Pallas kernels: none -> 560 us  [the longest x1 551 us: per_device(): pl.pallas_call(functools.partial(kernel, shards, groups), out_shape=(fina...]
    all_gather x2 -> x0, blocking collectives: 299 us -> none  [the longest x1 292 us: per_device(): row_router = lax.all_gather(part_router, 'shard', axis=0, tiled=True)]
    all_to_all x2 -> x0, waiting for transfers between devices: 252 us -> none  [the longest x1 252 us: per_device(): lax.all_to_all(narrow_gate, 'shard', split_axis=2, concat_axis=1, tiled=T...]
    all_to_all x4 -> x0, local copies, waits for them, and re-layouts: 67.1 us -> none  [the longest x2 33.6 us: per_device(): lax.all_to_all(narrow_up, 'shard', split_axis=2, concat_axis=1, tiled=True)]
    unnamed x7 -> x0, local copies, waits for them, and re-layouts: 43.7 us -> none
    all_to_all x2 -> x0, starting transfers between devices: 12.7 us -> none  [the longest x1 7.31 us: per_device(): lax.all_to_all(narrow_gate, 'shard', split_axis=2, concat_axis=1, tiled=T...]
  transfers between devices with their start and end apart: 2 -> 0, of which waited for: 1 -> 0; matrix products, arithmetic and copies ran while one was open for 5% -> 0% of each run, Pallas kernels for 0% -> 0%
where the time goes in v1:
time: 561 us
  Pallas kernels  560 us (100%)
    pallas_call x1, Pallas kernels, per_device(): pl.pallas_call(functools.partial(kernel, shards, groups), out_shape=(fina...  551 us

profile of v1, /device:TPU:0, one launch (start us, length us, event | category | flops | bytes accessed | tf_op | source)
XLA Modules:
  0.0 560.6 jit_solution(4085885789385316818)
XLA Ops:
  0.6 551.0 %shard_map.67 = (bf16[32,96,2048]{2,1,0:T(8,128)(2,1)S(1)}, bf16[32,96,2048]{2,1,0:T(8,128)(2,1)S(1)}, bf16[2048,128]{1,0:T(8,128)(2,1)S(1)}) custom-call(f32[32,256,768]{2,1,0:T(8,128)} %gate.1, f32[32,256,768]{2,1,0:T(8,128)} %up.1, f32[32,256]{1,0:T(8,128)} %bitcast.2, f32[1,256]{1,0:T(1,128)} %bitcast.3), custom_call_target="tpu_custom_call" | custom-call | tf_op jit(solution)/shard_map/pallas_call | solution.py:208
  551.6 8.9 %shard_map.68 = (bf16[32,96,2048]{2,1,0:T(8,128)(2,1)}, bf16[32,96,2048]{2,1,0:T(8,128)(2,1)}, bf16[2048,128]{1,0:T(8,128)(2,1)}) custom-call(bf16[32,96,2048]{2,1,0:T(8,128)(2,1)S(1)} %get-tuple-element.6.gate, bf16[32,96,2048]{2,1,0:T(8,128)(2,1)S(1)} %get-tuple-element.7.up, bf16[2048,128]{1,0:T(8,128)(2,1)S(1)} %get-tuple-element.8.router), custom_call_target="tpu_custom_call" | custom-call | tf_op jit(solution)/shard_map/pallas_call | solution.py:224
